TPU v7x, 32 devices: a whole 2x2x4 slice. The times are simulated.
32 devices in a mesh: ctx: 8 (over z, x), head: 4 (over y, core).
Axes of the slice: x: 2, y: 2, z: 4, core: 2. Of those that a mesh axis runs over, the one named last changes fastest.
Arguments:
- activations: bfloat16 [8192, 2048], P('ctx', 'head'), may hold values from -6 to 6
- w_query: bfloat16 [2048, 2048], P('ctx', 'head'), may hold values from -0.125 to 0.125
- w_key: bfloat16 [2048, 2048], P('ctx', 'head'), may hold values from -0.125 to 0.125
- w_value: bfloat16 [2048, 2048], P('ctx', 'head'), may hold values from -0.125 to 0.125
- level_table: float32 [16, 64, 14], P('head'), may hold values from 0.2 to 2
- table_rows: int32 [8192], P('ctx'), may hold values from 0 to 63
- out_grad: bfloat16 [8192, 2048], P('ctx', 'head'), may hold values from -0.059814453 to 0.059814453
Outputs:
- attended: bfloat16 [8192, 2048], P('ctx', 'head')
- grad_query: float32 [2048, 2048], P('ctx', 'head')
- grad_key: float32 [2048, 2048], P('ctx', 'head')
- grad_value: float32 [2048, 2048], P('ctx', 'head')
All inputs are finite; a program needn't handle non-finite values.
Results may differ from a plain program's by a relative error of at most 0.0056.
Values may be sent and summed in bfloat16 or wider, within the bound.
A program may use at most 64 MiB of HBM per device.

v0:
```python
import math

import jax
import jax.numpy as jnp
from jax import lax
from jax.sharding import PartitionSpec as P


def from_partner(block, axis, apart):
    count = lax.axis_size(axis)
    route = []
    for low in range(count):
        high = low | 1 << apart
        if high != low and high < count:
            route += [(low, high), (high, low)]
    return lax.ppermute(block, axis, route)


def level_of(distance, bit_total):
    running = jnp.zeros(distance.shape, jnp.int32)
    for bit_num in range(bit_total):
        running = running + (distance >= 1 << bit_num).astype(jnp.int32)
    return running


def on_device(activations, w_query, w_key, w_value, level_table, table_rows, out_grad):
    features = lax.all_gather(activations, "head", axis=1, tiled=True)
    row_count = features.shape[0]
    column_count = w_query.shape[1]
    heads_here = level_table.shape[0]
    table_size = level_table.shape[1]
    level_count = level_table.shape[2]
    head_width = column_count // heads_here
    inner_bits = row_count.bit_length() - 1
    outer_bits = lax.axis_size("ctx").bit_length() - 1
    my_index = lax.axis_index("ctx")
    scale_factor = 1.0 / math.sqrt(head_width * row_count)
    highest = lax.Precision.HIGHEST
    pieces = (
        lax.all_gather(w_query, "ctx", axis=0, tiled=True),
        lax.all_gather(w_key, "ctx", axis=0, tiled=True),
        lax.all_gather(w_value, "ctx", axis=0, tiled=True),
    )
    feature_cols = features
    projected = tuple(
        (
            jnp.dot(feature_cols, weight_piece, preferred_element_type=jnp.float32)
            for weight_piece in pieces
        )
    )
    queries = projected[0].astype(jnp.bfloat16).reshape(row_count, heads_here, head_width)
    key_proj = projected[1].astype(jnp.bfloat16).reshape(row_count, heads_here, head_width)
    value_proj = projected[2].astype(jnp.bfloat16).reshape(row_count, heads_here, head_width)
    grad_heads = out_grad.reshape(row_count, heads_here, head_width)
    onehot = (table_rows[:, None] == jnp.arange(table_size, dtype=jnp.int32)[None, :]).astype(
        jnp.float32
    )
    table_flat = jnp.transpose(level_table, (1, 0, 2)).reshape(table_size, heads_here * level_count)
    lam = jnp.dot(onehot, table_flat, precision=highest).reshape(row_count, heads_here, level_count)
    local_state = jnp.einsum(
        "thd,the->hde", key_proj, value_proj, preferred_element_type=jnp.float32
    )
    block_sum = local_state
    level_list = []
    for bit_num in range(outer_bits):
        sibling = from_partner(block_sum, "ctx", bit_num)
        is_upper = jnp.right_shift(my_index, bit_num) & 1 == 1
        level_list.append(jnp.where(is_upper, sibling, 0.0))
        block_sum = block_sum + sibling
    level_states = jnp.stack(level_list)
    state_narrow = level_states.astype(jnp.bfloat16)
    far_out = jnp.zeros((row_count, heads_here, head_width), jnp.float32)
    query_far = jnp.zeros((row_count, heads_here, head_width), jnp.float32)
    grad_list = []
    for bit_num in range(outer_bits):
        level_weight = lam[:, :, inner_bits + 1 + bit_num]
        far_out = far_out + scale_factor * level_weight[..., None] * jnp.einsum(
            "thd,hde->the", queries, state_narrow[bit_num], preferred_element_type=jnp.float32
        )
        query_far = query_far + scale_factor * level_weight[..., None] * jnp.einsum(
            "the,hde->thd", grad_heads, state_narrow[bit_num], preferred_element_type=jnp.float32
        )
        scaled_query = ((scale_factor * level_weight)[..., None] * queries).astype(jnp.bfloat16)
        grad_list.append(
            jnp.einsum("thd,the->hde", scaled_query, grad_heads, preferred_element_type=jnp.float32)
        )
    pending = jnp.stack(grad_list)
    incoming = jnp.zeros((heads_here, head_width, head_width), jnp.float32)
    for bit_num in range(outer_bits):
        partner = from_partner(pending[bit_num:], "ctx", bit_num)
        is_lower = jnp.right_shift(my_index, bit_num) & 1 == 0
        incoming = incoming + jnp.where(is_lower, partner[0], 0.0)
        pending = jnp.concatenate(
            [pending[: bit_num + 1], pending[bit_num + 1 :] + partner[1:]], axis=0
        )
    back_state = incoming.astype(jnp.bfloat16)
    key_far = jnp.einsum("the,hde->thd", value_proj, back_state, preferred_element_type=jnp.float32)
    value_far = jnp.einsum("thd,hde->the", key_proj, back_state, preferred_element_type=jnp.float32)
    positions = jnp.arange(row_count, dtype=jnp.int32)
    pair_level = level_of(jnp.bitwise_xor(positions[:, None], positions[None, :]), inner_bits + 1)
    causal = positions[:, None] >= positions[None, :]
    near_outs = []
    query_nears = []
    key_nears = []
    value_nears = []
    for head_idx in range(heads_here):
        level_mix = jnp.zeros((row_count, row_count), jnp.float32)
        for level_num in range(inner_bits + 1):
            level_mix = jnp.where(
                pair_level == level_num, lam[:, head_idx, level_num][:, None], level_mix
            )
        level_mix = jnp.where(causal, level_mix * scale_factor, 0.0)
        query_head = queries[:, head_idx]
        key_head = key_proj[:, head_idx]
        value_head = value_proj[:, head_idx]
        grad_head = grad_heads[:, head_idx]
        scores = jnp.dot(query_head, key_head.T, preferred_element_type=jnp.float32)
        attn_probs = (level_mix * scores).astype(jnp.bfloat16)
        near_outs.append(jnp.dot(attn_probs, value_head, preferred_element_type=jnp.float32))
        grad_scores = jnp.dot(grad_head, value_head.T, preferred_element_type=jnp.float32)
        grad_mixed = (level_mix * grad_scores).astype(jnp.bfloat16)
        query_nears.append(jnp.dot(grad_mixed, key_head, preferred_element_type=jnp.float32))
        key_nears.append(jnp.dot(grad_mixed.T, query_head, preferred_element_type=jnp.float32))
        value_nears.append(jnp.dot(attn_probs.T, grad_head, preferred_element_type=jnp.float32))
    attended = (
        (jnp.stack(near_outs, axis=1) + far_out)
        .astype(jnp.bfloat16)
        .reshape(row_count, column_count)
    )
    query_total = (
        (jnp.stack(query_nears, axis=1) + query_far)
        .astype(jnp.bfloat16)
        .reshape(row_count, column_count)
    )
    key_total = (
        (jnp.stack(key_nears, axis=1) + key_far)
        .astype(jnp.bfloat16)
        .reshape(row_count, column_count)
    )
    value_total = (
        (jnp.stack(value_nears, axis=1) + value_far)
        .astype(jnp.bfloat16)
        .reshape(row_count, column_count)
    )
    merged = jnp.concatenate([query_total, key_total, value_total], axis=1)
    feature_cols = features
    grad_all = lax.psum_scatter(
        jnp.dot(feature_cols.T, merged, preferred_element_type=jnp.float32),
        "ctx",
        scatter_dimension=0,
        tiled=True,
    )
    grad_query = grad_all[:, :column_count]
    grad_key = grad_all[:, column_count : 2 * column_count]
    grad_value = grad_all[:, 2 * column_count :]
    return (attended, grad_query, grad_key, grad_value)


def solution(mesh):
    return jax.shard_map(
        on_device,
        mesh=mesh,
        in_specs=(
            P("ctx", "head"),
            P("ctx", "head"),
            P("ctx", "head"),
            P("ctx", "head"),
            P("head", None, None),
            P("ctx"),
            P("ctx", "head"),
        ),
        out_specs=(P("ctx", "head"), P("ctx", "head"), P("ctx", "head"), P("ctx", "head")),
        check_vma=False,
    )
```

profile of v0, /device:TPU:0, one launch (start us, length us, event | category | flops | bytes accessed | tf_op | source)
XLA Modules:
  0.0 552.3 jit_solution(5934484398656798456)
XLA Ops:
  14.7 47.3 %all-gather.9.cloned.1.call-done = bf16[2048,512]{1,0:T(8,128)(2,1)} async-done(((bf16[256,512]{1,0:T(8,128)(2,1)}), bf16[2048,512]{1,0:T(8,128)(2,1)}) %all-gather.9.cloned.1.call-update) | async-done | bytes 2097168 | tf_op jit(solution)/shard_map/all_gather | solution.py:41
  61.9 34.6 %all-gather.5.cloned.1.call-done = bf16[1024,2048]{1,0:T(8,128)(2,1)} async-done(((bf16[1024,512]{1,0:T(8,128)(2,1)}), bf16[1024,2048]{1,0:T(8,128)(2,1)}) %all-gather.5.cloned.1.call-update) | async-done | bytes 4194320 | tf_op jit(solution)/shard_map/all_gather | solution.py:27
  96.5 5.2 convolution_convert_fusion.1
  101.8 46.0 %all-gather.11.cloned.1.call-done = bf16[2048,512]{1,0:T(8,128)(2,1)} async-done(((bf16[256,512]{1,0:T(8,128)(2,1)}), bf16[2048,512]{1,0:T(8,128)(2,1)}) %all-gather.11.cloned.1.call-update) | async-done | bytes 2097168 | tf_op jit(solution)/shard_map/all_gather | solution.py:42
  147.8 5.2 convolution_convert_fusion
  153.0 9.0 %fusion = bf16[1024,1024]{1,0:T(8,128)(2,1)S(1)} fusion(f32[1024]{0:T(1024)S(1)} %bitcast.392, f32[1024]{0:T(1024)S(1)} %bitcast.394, f32[1024]{0:T(1024)S(1)} %bitcast.396, f32[1024]{0:T(1024)S(1)} %bitcast.398, f32[1024]{0:T(1024)S(1)} %bitcast.400, f32[1024]{0:T(1024)S(1)} %bitcast.402, f32[1024]{0:T(1024)S(1)} %bitcast.404, f32[1024]{0:T(1024)S(1)} %bitcast.406, ...), kind=kOutput, calls=%fused_computation.2 | convolution fusion | flops 331350016 | bytes 2666496 | tf_op jit(solution)/shard_map/dot_general | solution.py:120
  163.4 1.6 convolution_bitcast_fusion.9
  166.2 31.5 %all-gather.7.cloned.1.call-done = bf16[2048,512]{1,0:T(8,128)(2,1)} async-done(((bf16[256,512]{1,0:T(8,128)(2,1)}), bf16[2048,512]{1,0:T(8,128)(2,1)}) %all-gather.7.cloned.1.call-update) | async-done | bytes 2097168 | tf_op jit(solution)/shard_map/all_gather | solution.py:40
  197.7 5.4 convolution_convert_fusion.2
  203.5 9.2 %multiply_convert_fusion = bf16[1024,1024]{1,0:T(8,128)(2,1)S(1)} fusion(f32[1024]{0:T(1024)S(1)} %bitcast.393, f32[1024]{0:T(1024)S(1)} %bitcast.395, f32[1024]{0:T(1024)S(1)} %bitcast.397, f32[1024]{0:T(1024)S(1)} %bitcast.399, f32[1024]{0:T(1024)S(1)} %bitcast.401, f32[1024]{0:T(1024)S(1)} %bitcast.403, f32[1024]{0:T(1024)S(1)} %bitcast.405, ...), kind=kOutput, calls=%fused_computation.9 | convolution fusion | flops 331350016 | bytes 2666496 | tf_op jit(solution)/shard_map/dot_general | solution.py:117
  212.7 9.0 %fusion.1 = bf16[1024,1024]{1,0:T(8,128)(2,1)S(1)} fusion(f32[1024]{0:T(1024)S(1)} %bitcast.378, f32[1024]{0:T(1024)S(1)} %bitcast.380, f32[1024]{0:T(1024)S(1)} %bitcast.382, f32[1024]{0:T(1024)S(1)} %bitcast.384, f32[1024]{0:T(1024)S(1)} %bitcast.386, f32[1024]{0:T(1024)S(1)} %bitcast.388, f32[1024]{0:T(1024)S(1)} %bitcast.390, f32[1024]{0:T(1024)S(1)} %bitcast.356, ...), kind=kOutput, calls=%fused_computation.4 | convolution fusion | flops 331350016 | bytes 2666496 | tf_op jit(solution)/shard_map/dot_general | solution.py:120
  223.0 9.0 %multiply_convert_fusion.1 = bf16[1024,1024]{1,0:T(8,128)(2,1)S(1)} fusion(f32[1024]{0:T(1024)S(1)} %bitcast.379, f32[1024]{0:T(1024)S(1)} %bitcast.381, f32[1024]{0:T(1024)S(1)} %bitcast.383, f32[1024]{0:T(1024)S(1)} %bitcast.385, f32[1024]{0:T(1024)S(1)} %bitcast.387, f32[1024]{0:T(1024)S(1)} %bitcast.389, f32[1024]{0:T(1024)S(1)} %bitcast.391, ...), kind=kOutput, calls=%fused_computation.11 | convolution fusion | flops 331350016 | bytes 2666496 | tf_op jit(solution)/shard_map/dot_general | solution.py:117
  232.0 9.0 %fusion.2 = bf16[1024,1024]{1,0:T(8,128)(2,1)S(1)} fusion(f32[1024]{0:T(1024)S(1)} %bitcast.334, f32[1024]{0:T(1024)S(1)} %bitcast.336, f32[1024]{0:T(1024)S(1)} %bitcast.338, f32[1024]{0:T(1024)S(1)} %bitcast.340, f32[1024]{0:T(1024)S(1)} %bitcast.342, f32[1024]{0:T(1024)S(1)} %bitcast.344, f32[1024]{0:T(1024)S(1)} %bitcast.346, f32[1024]{0:T(1024)S(1)} %bitcast.348, ...), kind=kOutput, calls=%fused_computation.6 | convolution fusion | flops 331350016 | bytes 2666496 | tf_op jit(solution)/shard_map/dot_general | solution.py:120
  241.0 9.2 %multiply_convert_fusion.2 = bf16[1024,1024]{1,0:T(8,128)(2,1)S(1)} fusion(f32[1024]{0:T(1024)S(1)} %bitcast.335, f32[1024]{0:T(1024)S(1)} %bitcast.337, f32[1024]{0:T(1024)S(1)} %bitcast.339, f32[1024]{0:T(1024)S(1)} %bitcast.341, f32[1024]{0:T(1024)S(1)} %bitcast.343, f32[1024]{0:T(1024)S(1)} %bitcast.345, f32[1024]{0:T(1024)S(1)} %bitcast.347, ...), kind=kOutput, calls=%fused_computation.13 | convolution fusion | flops 331350016 | bytes 2666496 | tf_op jit(solution)/shard_map/dot_general | solution.py:117
  250.2 9.0 %fusion.3 = bf16[1024,1024]{1,0:T(8,128)(2,1)S(1)} fusion(f32[1024]{0:T(1024)S(1)} %bitcast.328, f32[1024]{0:T(1024)S(1)} %bitcast.330, f32[1024]{0:T(1024)S(1)} %bitcast.332, f32[1024]{0:T(1024)S(1)} %bitcast.368, f32[1024]{0:T(1024)S(1)} %bitcast.370, f32[1024]{0:T(1024)S(1)} %bitcast.372, f32[1024]{0:T(1024)S(1)} %bitcast.374, f32[1024]{0:T(1024)S(1)} %bitcast.376, ...), kind=kOutput, calls=%fused_computation.8 | convolution fusion | flops 331350016 | bytes 2666496 | tf_op jit(solution)/shard_map/dot_general | solution.py:120
  259.2 9.2 %multiply_convert_fusion.3 = bf16[1024,1024]{1,0:T(8,128)(2,1)S(1)} fusion(f32[1024]{0:T(1024)S(1)} %bitcast.329, f32[1024]{0:T(1024)S(1)} %bitcast.331, f32[1024]{0:T(1024)S(1)} %bitcast.333, f32[1024]{0:T(1024)S(1)} %bitcast.369, f32[1024]{0:T(1024)S(1)} %bitcast.371, f32[1024]{0:T(1024)S(1)} %bitcast.373, f32[1024]{0:T(1024)S(1)} %bitcast.375, ...), kind=kOutput, calls=%fused_computation.15 | convolution fusion | flops 331350016 | bytes 2666496 | tf_op jit(solution)/shard_map/dot_general | solution.py:117
  279.4 12.2 %collective-permute-done.3 = f32[3,4,128,128]{3,2,1,0:T(8,128)S(1)} collective-permute-done((f32[3,4,128,128]{3,2,1,0:T(8,128)S(1)}, f32[3,4,128,128]{3,2,1,0:T(8,128)S(1)}, u32[]{:S(2)}, u32[]{:S(2)}) %collective-permute-start.3) | collective-permute-done | bytes 786464 | tf_op jit(solution)/shard_map/ppermute | solution.py:16
  291.7 2.4 collective-permute-start.4
  296.5 10.4 %collective-permute-done.4 = f32[2,4,128,128]{3,2,1,0:T(8,128)S(1)} collective-permute-done((f32[2,4,128,128]{3,2,1,0:T(8,128)S(1)}, f32[2,4,128,128]{3,2,1,0:T(8,128)S(1)}, u32[]{:S(2)}, u32[]{:S(2)}) %collective-permute-start.4) | collective-permute-done | bytes 524320 | tf_op jit(solution)/shard_map/ppermute | solution.py:16
  309.3 11.1 %collective-permute-done.5 = f32[1,4,128,128]{3,2,1,0:T(8,128)S(1)} collective-permute-done((f32[1,4,128,128]{3,2,1,0:T(8,128)S(1)}, f32[1,4,128,128]{3,2,1,0:T(8,128)S(1)}, u32[]{:S(2)}, u32[]{:S(2)}) %collective-permute-start.5) | collective-permute-done | bytes 262176 | tf_op jit(solution)/shard_map/ppermute | solution.py:16
  322.6 12.2 %convolution_bitcast_fusion = f32[2048,1536]{0,1:T(8,128)} fusion(bf16[1024,2048]{1,0:T(8,128)(2,1)S(1)} %copy-done.19, bf16[1024,512]{0,1:T(8,128)(2,1)S(1)} %bitcast.415, bf16[1024,512]{0,1:T(8,128)(2,1)S(1)} %bitcast.414, bf16[1024,512]{0,1:T(8,128)(2,1)S(1)} %bitcast.320), kind=kOutput, calls=%fused_computation | convolution fusion | flops 6451888128 | bytes 19922944 | tf_op jit(solution)/shard_map/dot_general | solution.py:148
  334.8 2.6 convolution_bitcast_fusion.13
  337.4 2.4 convolution_bitcast_fusion.14
  344.8 196.1 %reduce-scatter.2.cloned.1.call-done = f32[256,1536]{0,1:T(8,128)} async-done(((f32[2048,1536]{0,1:T(8,128)}), f32[256,1536]{0,1:T(8,128)}) %reduce-scatter.2.cloned.1.call-update) | async-done | bytes 1572880 | tf_op jit(solution)/shard_map/reduce_scatter | solution.py:147
  (105 shorter events, 38.7 us)
Async XLA Ops:
  7.2 54.8 %all-gather.9.cloned.1.call-start = ((), (), s32[]{:S(2)}) async-start(), calls=%async_computation.3 | async-start | bytes 2359296 | tf_op jit(solution)/shard_map/all_gather | solution.py:41
  7.9 88.6 %all-gather.5.cloned.1.call-start = ((), (), s32[]{:S(2)}) async-start(), calls=%async_computation.1 | async-start | bytes 5242880 | tf_op jit(solution)/shard_map/all_gather | solution.py:27
  8.6 139.1 %all-gather.11.cloned.1.call-start = ((), (), s32[]{:S(2)}) async-start(), calls=%async_computation.4 | async-start | bytes 2359296 | tf_op jit(solution)/shard_map/all_gather | solution.py:42
  9.4 188.3 %all-gather.7.cloned.1.call-start = ((), (), s32[]{:S(2)}) async-start(), calls=%async_computation.2 | async-start | bytes 2359296 | tf_op jit(solution)/shard_map/all_gather | solution.py:40
  10.0 530.9 %reduce-scatter.2.cloned.1.call-start = ((), (), s32[]{:S(2)}) async-start(), calls=%async_computation.5 | async-start | bytes 14155776 | tf_op jit(solution)/shard_map/reduce_scatter | solution.py:147
  101.8 63.3 %copy-start.8 = (bf16[1024,512]{0,1:T(8,128)(2,1)}, bf16[1024,512]{0,1:T(8,128)(2,1)S(1)}, u32[]{:S(2)}) copy-start(bf16[1024,512]{0,1:T(8,128)(2,1)S(1)} %convolution_convert_fusion.1) | copy-start | bytes 3145732
  197.7 5.4 copy-start.7
  197.7 5.8 %copy-start.9 = (bf16[1024,512]{0,1:T(8,128)(2,1)S(1)}, bf16[1024,512]{0,1:T(8,128)(2,1)}, u32[]{:S(2)}) copy-start(bf16[1024,512]{0,1:T(8,128)(2,1)} %copy-done.8) | copy-start | bytes 3145732
  212.7 59.4 %copy-start = (bf16[1024,1024]{1,0:T(8,128)(2,1)}, bf16[1024,1024]{1,0:T(8,128)(2,1)S(1)}, u32[]{:S(2)}) copy-start(bf16[1024,1024]{1,0:T(8,128)(2,1)S(1)} %multiply_convert_fusion) | copy-start | bytes 6291460
  232.0 40.6 %copy-start.1 = (bf16[1024,1024]{1,0:T(8,128)(2,1)}, bf16[1024,1024]{1,0:T(8,128)(2,1)S(1)}, u32[]{:S(2)}) copy-start(bf16[1024,1024]{1,0:T(8,128)(2,1)S(1)} %multiply_convert_fusion.1) | copy-start | bytes 6291460
  250.2 23.3 %copy-start.2 = (bf16[1024,1024]{1,0:T(8,128)(2,1)}, bf16[1024,1024]{1,0:T(8,128)(2,1)S(1)}, u32[]{:S(2)}) copy-start(bf16[1024,1024]{1,0:T(8,128)(2,1)S(1)} %multiply_convert_fusion.2) | copy-start | bytes 6291460
  259.2 9.3 %copy-start.13 = (f32[4,128,128]{2,1,0:T(8,128)S(1)}, f32[4,128,128]{2,1,0:T(8,128)}, u32[]{:S(2)}) copy-start(f32[4,128,128]{2,1,0:T(8,128)} %fusion.60) | copy-start | bytes 786436
  259.2 9.9 %copy-start.15 = (f32[1024,4]{0,1:T(4,128)S(1)}, f32[1024,4]{0,1:T(4,128)}, u32[]{:S(2)}) copy-start(f32[1024,4]{0,1:T(4,128)} %get-tuple-element.66) | copy-start | bytes 49156
  259.2 10.4 %copy-start.17 = (f32[1024,4]{0,1:T(4,128)S(1)}, f32[1024,4]{0,1:T(4,128)}, u32[]{:S(2)}) copy-start(f32[1024,4]{0,1:T(4,128)} %get-tuple-element.67) | copy-start | bytes 49156
  268.5 6.8 %copy-start.4 = (bf16[1024,1024]{1,0:T(8,128)(2,1)}, bf16[1024,1024]{1,0:T(8,128)(2,1)S(1)}, u32[]{:S(2)}) copy-start(bf16[1024,1024]{1,0:T(8,128)(2,1)S(1)} %multiply_convert_fusion.3) | copy-start | bytes 6291460
  268.5 9.2 %collective-permute-start = (f32[4,128,128]{2,1,0:T(8,128)S(1)}, f32[4,128,128]{2,1,0:T(8,128)S(1)}, u32[]{:S(2)}, u32[]{:S(2)}) collective-permute-start(f32[4,128,128]{2,1,0:T(8,128)S(1)} %copy-done.13), channel_id=1, source_target_pairs={{0,4},{4,0},{8,12},{12,8},{16,20},{20,16},{24,28},{28,24},{1,5},{5... | collective-permute-start | bytes 786440 | tf_op jit(solution)/shard_map/ppermute | solution.py:16
  270.6 21.0 %collective-permute-start.3 = (f32[3,4,128,128]{3,2,1,0:T(8,128)S(1)}, f32[3,4,128,128]{3,2,1,0:T(8,128)S(1)}, u32[]{:S(2)}, u32[]{:S(2)}) collective-permute-start(f32[3,4,128,128]{3,2,1,0:T(8,128)S(1)} %pad_maximum_fusion), channel_id=1, source_target_pairs={{0,4},{4,0},{8,12},{12,8},{16,20},{20,16},{24,28},{28,24},{1,5},{5... | collective-permute-start | bytes 2359304 | tf_op jit(solution)/shard_map/ppermute | solution.py:16
  277.8 16.7 %collective-permute-start.1 = (f32[4,128,128]{2,1,0:T(8,128)S(1)}, f32[4,128,128]{2,1,0:T(8,128)S(1)}, u32[]{:S(2)}, u32[]{:S(2)}) collective-permute-start(f32[4,128,128]{2,1,0:T(8,128)S(1)} %add.946), channel_id=1, source_target_pairs={{0,8},{8,0},{4,12},{12,4},{16,24},{24,16},{20,28},{28,20},{1,9},{9... | collective-permute-start | bytes 786440 | tf_op jit(solution)/shard_map/ppermute | solution.py:16
  291.6 16.7 %copy-start.12 = (f32[1024,1,128]{0,2,1:T(8,128)S(1)}, f32[1024,1,128]{0,2,1:T(8,128)}, u32[]{:S(2)}) copy-start(f32[1024,1,128]{0,2,1:T(8,128)} %convolution_bitcast_fusion.9) | copy-start | bytes 1572868
  291.7 15.2 %collective-permute-start.4 = (f32[2,4,128,128]{3,2,1,0:T(8,128)S(1)}, f32[2,4,128,128]{3,2,1,0:T(8,128)S(1)}, u32[]{:S(2)}, u32[]{:S(2)}) collective-permute-start(f32[2,4,128,128]{3,2,1,0:T(8,128)S(1)} %slice_add_fusion), channel_id=1, source_target_pairs={{0,8},{8,0},{4,12},{12,4},{16,24},{24,16},{20,28},{28,20},{1,9},{9... | collective-permute-start | bytes 1572872 | tf_op jit(solution)/shard_map/ppermute | solution.py:16
  294.5 14.7 %copy-start.10 = (f32[4,128,128]{2,1,0:T(8,128)}, f32[4,128,128]{2,1,0:T(8,128)S(1)}, u32[]{:S(2)}) copy-start(f32[4,128,128]{2,1,0:T(8,128)S(1)} %collective-permute-done.1) | copy-start | bytes 786436
  294.6 13.8 %collective-permute-start.2 = (bf16[4,128,128]{2,1,0:T(8,128)(2,1)S(1)}, bf16[4,128,128]{2,1,0:T(8,128)(2,1)S(1)}, u32[]{:S(2)}, u32[]{:S(2)}) collective-permute-start(bf16[4,128,128]{2,1,0:T(8,128)(2,1)S(1)} %add.948), channel_id=1, source_target_pairs={{0,16},{16,0},{4,20},{20,4},{8,24},{24,8},{12,28},{28,12},{1,17},{... | collective-permute-start | bytes 393224 | tf_op jit(solution)/shard_map/ppermute | solution.py:16
  306.9 13.4 %collective-permute-start.5 = (f32[1,4,128,128]{3,2,1,0:T(8,128)S(1)}, f32[1,4,128,128]{3,2,1,0:T(8,128)S(1)}, u32[]{:S(2)}, u32[]{:S(2)}) collective-permute-start(f32[1,4,128,128]{3,2,1,0:T(8,128)S(1)} %slice_add_fusion.1), channel_id=1, source_target_pairs={{0,16},{16,0},{4,20},{20,4},{8,24},{24,8},{12,28},{28,12},{1,17},{... | collective-permute-start | bytes 786440 | tf_op jit(solution)/shard_map/ppermute | solution.py:16
  334.8 5.9 %copy-start.5 = (bf16[1024,1024]{1,0:T(8,128)(2,1)S(1)}, bf16[1024,1024]{1,0:T(8,128)(2,1)}, u32[]{:S(2)}) copy-start(bf16[1024,1024]{1,0:T(8,128)(2,1)} %copy-done.4) | copy-start | bytes 6291460
  (7 other events, 16.1 us)
Sparse Core Ops, SparseCore 0:
  10.1 51.7 all-gather.8
  63.5 32.9 all-gather.4
  98.7 49.0 all-gather.10
  149.8 47.8 all-gather.6
  334.9 205.8 reduce-scatter.1
where the time goes:
time: 560 us; the launch traced here: 552 us
  waiting for transfers between devices  393 us (70%)
  matrix products  123 us (22%)
  between operations  14.9 us (3%)
  local copies, waits for them, and re-layouts  12.1 us (2%)
  starting transfers between devices  9.29 us (2%)
    reduce_scatter x1, waiting for transfers between devices, on_device(): lax.psum_scatter(jnp.dot(feature_cols.T, merged, preferred_element_type=j...  196 us
    all_gather x1, waiting for transfers between devices, on_device(): lax.all_gather(w_key, 'ctx', axis=0, tiled=True)  47.3 us
    all_gather x1, waiting for transfers between devices, on_device(): lax.all_gather(w_value, 'ctx', axis=0, tiled=True)  46 us
    dot_general x4, matrix products, on_device(): scores = jnp.dot(query_head, key_head.T, preferred_element_type=jnp.float32)  36.6 us
    dot_general x4, matrix products, on_device(): jnp.dot(grad_head, value_head.T, preferred_element_type=jnp.float32)  35.9 us
    ppermute x6, waiting for transfers between devices, from_partner(): return lax.ppermute(block, axis, route)  34.8 us
    all_gather x1, waiting for transfers between devices, on_device(): features = lax.all_gather(activations, 'head', axis=1, tiled=True)  34.6 us
    all_gather x1, waiting for transfers between devices, on_device(): lax.all_gather(w_query, 'ctx', axis=0, tiled=True)  31.5 us
  transfers between devices with their start and end apart: 11, of which 9 were waited for; matrix products, arithmetic and copies ran while one was open for 8% of the time, Pallas kernels for 0%

commit v1 on v0

v1 whole, which is shorter than its diff:
```python
import functools
import math

import jax
import jax.numpy as jnp
from jax import lax
from jax.experimental import pallas as pl
from jax.experimental.pallas import tpu as pltpu
from jax.sharding import PartitionSpec as P

F32 = jnp.float32
BF16 = jnp.bfloat16


def mm(a, b, ca, cb):
    return lax.dot_general(a, b, (((ca,), (cb,)), ((), ())), preferred_element_type=F32)


def from_partner(block, axis, apart):
    count = lax.axis_size(axis)
    route = []
    for low in range(count):
        high = low | 1 << apart
        if high != low and high < count:
            route += [(low, high), (high, low)]
    return lax.ppermute(block, axis, route)


def state_kernel(first_far, outer_bits, q_ref, k_ref, v_ref, g_ref, lam_ref, out_ref):
    q = q_ref[...].astype(F32)
    g = g_ref[...]
    out_ref[0, 0] = mm(k_ref[...], v_ref[...], 0, 0)
    for b in range(outer_bits):
        level = first_far + b
        scaled = (lam_ref[0, :, level : level + 1] * q).astype(BF16)
        out_ref[1 + b, 0] = mm(scaled, g, 0, 0)


def near_kernel(tile, inner_bits, q_ref, k_ref, v_ref, g_ref, lam_ref, out_ref, qn_ref, kn_ref, vn_ref):
    rows, width = q_ref.shape
    chunks = rows // tile
    tile_bits = tile.bit_length() - 1
    r = lax.broadcasted_iota(jnp.int32, (tile, tile), 0)
    s = lax.broadcasted_iota(jnp.int32, (tile, tile), 1)
    apart = jnp.where(r >= s, r ^ s, -1)
    spans = inner_bits - tile_bits
    states = []
    grads = {}
    for c in range(chunks):
        at = pl.ds(c * tile, tile)
        q, k, v, g = q_ref[at], k_ref[at], v_ref[at], g_ref[at]
        if spans:
            states.append(mm(k, v, 0, 0))
        for b in range(spans):
            if c >> b & 1:
                level = tile_bits + 1 + b
                scaled = (lam_ref[0, at, level : level + 1] * q.astype(F32)).astype(BF16)
                grads[b, c] = mm(scaled, g, 0, 0)
    for c in range(chunks):
        at = pl.ds(c * tile, tile)
        q, k, v, g = q_ref[at], k_ref[at], v_ref[at], g_ref[at]
        mix = jnp.where(apart >= 0, lam_ref[0, at, 0:1], 0.0)
        for level in range(1, tile_bits + 1):
            mix = jnp.where(apart >= 1 << (level - 1), lam_ref[0, at, level : level + 1], mix)
        probs = (mix * mm(q, k, 1, 1)).astype(BF16)
        mixed = (mix * mm(g, v, 1, 1)).astype(BF16)
        near = mm(probs, v, 1, 0)
        qn = mm(mixed, k, 1, 0)
        kn = mm(mixed, q, 0, 0)
        vn = mm(probs, g, 0, 0)
        back = None
        for b in range(spans):
            sibling = (c >> b) ^ 1
            members = range(sibling << b, (sibling + 1) << b)
            if c >> b & 1:
                level = tile_bits + 1 + b
                state = sum(states[e] for e in members).astype(BF16)
                weight = lam_ref[0, at, level : level + 1]
                near = near + weight * mm(q, state, 1, 0)
                qn = qn + weight * mm(g, state, 1, 1)
            else:
                part = sum(grads[b, e] for e in members)
                back = part if back is None else back + part
        if back is not None:
            back = back.astype(BF16)
            kn = kn + mm(v, back, 1, 1)
            vn = vn + mm(k, back, 1, 0)
        out_ref[at] = near
        qn_ref[at] = qn
        kn_ref[at] = kn
        vn_ref[at] = vn


def far_kernel(first_far, outer_bits, q_ref, k_ref, v_ref, g_ref, lam_ref, st_ref, back_ref,
               near_ref, qn_ref, kn_ref, vn_ref, out_ref, qt_ref, kt_ref, vt_ref):
    q, k, v, g = q_ref[...], k_ref[...], v_ref[...], g_ref[...]
    near = near_ref[...]
    qn = qn_ref[...]
    for b in range(outer_bits):
        level = first_far + b
        weight = lam_ref[0, :, level : level + 1]
        state = st_ref[b, 0]
        near = near + weight * mm(q, state, 1, 0)
        qn = qn + weight * mm(g, state, 1, 1)
    out_ref[...] = near.astype(BF16)
    qt_ref[...] = qn.astype(BF16)
    back = back_ref[0]
    kt_ref[...] = (kn_ref[...] + mm(v, back, 1, 1)).astype(BF16)
    vt_ref[...] = (vn_ref[...] + mm(k, back, 1, 0)).astype(BF16)


def on_device(activations, w_query, w_key, w_value, level_table, table_rows, out_grad):
    features = lax.all_gather(activations, "head", axis=1, tiled=True)
    rows = features.shape[0]
    columns = w_query.shape[1]
    heads, table_size, level_count = level_table.shape
    width = columns // heads
    inner_bits = rows.bit_length() - 1
    outer_bits = lax.axis_size("ctx").bit_length() - 1
    first_far = inner_bits + 1
    tile = min(256, rows)
    my_index = lax.axis_index("ctx")
    scale = 1.0 / math.sqrt(width * rows)
    onehot = (table_rows[:, None] == jnp.arange(table_size, dtype=jnp.int32)[None, :]).astype(F32)
    lam = scale * jnp.einsum("tr,hrl->htl", onehot, level_table, precision=lax.Precision.HIGHEST)

    def project(w):
        whole = lax.all_gather(w, "ctx", axis=0, tiled=True)
        return jnp.dot(features, whole, preferred_element_type=F32).astype(BF16)

    key = project(w_key)
    value = project(w_value)
    query = project(w_query)

    col = pl.BlockSpec((rows, width), lambda h: (0, h))
    lam_spec = pl.BlockSpec((1, rows, level_count), lambda h: (h, 0, 0))
    packed = pl.pallas_call(
        functools.partial(state_kernel, first_far, outer_bits),
        grid=(heads,),
        in_specs=[col] * 4 + [lam_spec],
        out_specs=pl.BlockSpec((1 + outer_bits, 1, width, width), lambda h: (0, h, 0, 0)),
        out_shape=jax.ShapeDtypeStruct((1 + outer_bits, heads, width, width), F32),
        cost_estimate=pl.CostEstimate(
            flops=2 * rows * columns * width * (1 + outer_bits),
            bytes_accessed=8 * rows * columns, transcendentals=0),
    )(query, key, value, out_grad, lam)

    near_parts = pl.pallas_call(
        functools.partial(near_kernel, tile, inner_bits),
        grid=(heads,),
        in_specs=[col] * 4 + [lam_spec],
        out_specs=[col] * 4,
        out_shape=[jax.ShapeDtypeStruct((rows, columns), F32)] * 4,
        cost_estimate=pl.CostEstimate(
            flops=24 * rows * columns * tile,
            bytes_accessed=24 * rows * columns, transcendentals=0),
    )(query, key, value, out_grad, lam)

    block_sum = packed[0]
    pending = packed[1:]
    incoming = jnp.zeros((heads, width, width), F32)
    levels = []
    for b in range(outer_bits):
        sent = jnp.concatenate([block_sum[None], pending[b:]], axis=0).astype(BF16)
        got = from_partner(sent, "ctx", b).astype(F32)
        is_upper = jnp.right_shift(my_index, b) & 1 == 1
        levels.append(jnp.where(is_upper, got[0], 0.0).astype(BF16))
        incoming = incoming + jnp.where(is_upper, 0.0, got[1])
        if b + 1 < outer_bits:
            block_sum = block_sum + got[0]
            pending = jnp.concatenate([pending[: b + 1], pending[b + 1 :] + got[2:]], axis=0)
    states = jnp.stack(levels)
    back = incoming.astype(BF16)

    attended, q_total, k_total, v_total = pl.pallas_call(
        functools.partial(far_kernel, first_far, outer_bits),
        grid=(heads,),
        in_specs=[col] * 4 + [
            lam_spec,
            pl.BlockSpec((outer_bits, 1, width, width), lambda h: (0, h, 0, 0)),
            pl.BlockSpec((1, width, width), lambda h: (h, 0, 0)),
        ] + [col] * 4,
        out_specs=[col] * 4,
        out_shape=[jax.ShapeDtypeStruct((rows, columns), BF16)] * 4,
        cost_estimate=pl.CostEstimate(
            flops=4 * rows * columns * width * (1 + outer_bits),
            bytes_accessed=32 * rows * columns, transcendentals=0),
    )(query, key, value, out_grad, lam, states, back, *near_parts)

    def gradient(total):
        share = mm(features, total, 0, 0).astype(BF16)
        return lax.psum_scatter(share, "ctx", scatter_dimension=0, tiled=True).astype(F32)

    return attended, gradient(q_total), gradient(k_total), gradient(v_total)


def solution(mesh):
    return jax.shard_map(
        on_device,
        mesh=mesh,
        in_specs=(
            P("ctx", "head"),
            P("ctx", "head"),
            P("ctx", "head"),
            P("ctx", "head"),
            P("head", None, None),
            P("ctx"),
            P("ctx", "head"),
        ),
        out_specs=(P("ctx", "head"), P("ctx", "head"), P("ctx", "head"), P("ctx", "head")),
        check_vma=False,
    )
```

time: 560 us -> 489 us (0.87); the launches traced: 552 us -> 489 us
  matrix products: 123 us -> 39.8 us
  Pallas kernels: 0 us -> 28.8 us
    dot_general x41 -> x7, matrix products: 123 us -> 39.8 us  [the longest x3 18.5 us: project(): return jnp.dot(features, whole, preferred_element_type=F32).astype(BF16)]
    pallas_call x0 -> x3, Pallas kernels: none -> 28.8 us  [the longest x1 13.6 us: on_device(): pl.pallas_call(functools.partial(near_kernel, tile, inner_bits), grid=(he...]
    ppermute x6 -> x3, waiting for transfers between devices: 34.8 us -> 21.9 us  [from_partner(): return lax.ppermute(block, axis, route)]
    all_gather x3, waiting for transfers between devices: 125 us -> 137 us  [project(): whole = lax.all_gather(w, 'ctx', axis=0, tiled=True)]
    reduce_scatter x1 -> x3, waiting for transfers between devices: 196 us -> 193 us  [gradient(): lax.psum_scatter(share, 'ctx', scatter_dimension=0, tiled=True).astype(F32)]
  transfers between devices with their start and end apart: 11 -> 10, of which waited for: 9 -> 9; matrix products, arithmetic and copies ran while one was open for 8% -> 6% of each run, Pallas kernels for 0% -> 3%
where the time goes in v1:
time: 489 us
  waiting for transfers between devices  390 us (80%)
  matrix products  39.8 us (8%)
  Pallas kernels  28.8 us (6%)
  between operations  14.2 us (3%)
  local copies, waits for them, and re-layouts  7.75 us (2%)
  starting transfers between devices  5.02 us (1%)
    reduce_scatter x3, waiting for transfers between devices, gradient(): lax.psum_scatter(share, 'ctx', scatter_dimension=0, tiled=True).astype(F32)  193 us
    all_gather x3, waiting for transfers between devices, project(): whole = lax.all_gather(w, 'ctx', axis=0, tiled=True)  137 us
    all_gather x1, waiting for transfers between devices, on_device(): features = lax.all_gather(activations, 'head', axis=1, tiled=True)  34.6 us
    ppermute x3, waiting for transfers between devices, from_partner(): return lax.ppermute(block, axis, route)  21.9 us
    dot_general x3, matrix products, project(): return jnp.dot(features, whole, preferred_element_type=F32).astype(BF16)  18.5 us
    dot_general x3, matrix products, mm(): lax.dot_general(a, b, (((ca,), (cb,)), ((), ())), preferred_element_type=...  18.2 us
    pallas_call x1, Pallas kernels, on_device(): pl.pallas_call(functools.partial(near_kernel, tile, inner_bits), grid=(he...  13.6 us
  transfers between devices with their start and end apart: 10, of which 9 were waited for; matrix products, arithmetic and copies ran while one was open for 6% of the time, Pallas kernels for 3%

profile of v1, /device:TPU:0, one launch (start us, length us, event | category | flops | bytes accessed | tf_op | source)
XLA Modules:
  0.0 488.8 jit_solution(18387828055729508045)
XLA Ops:
  10.0 3.1 multiply_bitcast_fusion.lam_ref
  13.1 48.8 %all-gather.7.cloned.1.call-done = bf16[2048,512]{1,0:T(8,128)(2,1)} async-done(((bf16[256,512]{1,0:T(8,128)(2,1)}), bf16[2048,512]{1,0:T(8,128)(2,1)}) %all-gather.7.cloned.1.call-update) | async-done | bytes 2097168 | tf_op jit(solution)/shard_map/all_gather | solution.py:128
  62.0 34.6 %all-gather.5.cloned.1.call-done = bf16[1024,2048]{1,0:T(8,128)(2,1)} async-done(((bf16[1024,512]{1,0:T(8,128)(2,1)}), bf16[1024,2048]{1,0:T(8,128)(2,1)}) %all-gather.5.cloned.1.call-update) | async-done | bytes 4194320 | tf_op jit(solution)/shard_map/all_gather | solution.py:113
  96.5 6.2 %convolution_convert_fusion.5.q_ref = bf16[1024,512]{1,0:T(8,128)(2,1)} fusion(bf16[1024,2048]{1,0:T(8,128)(2,1)} %all-gather.5.cloned.1.call-done, bf16[2048,512]{1,0:T(8,128)(2,1)} %all-gather.7.cloned.1.call-done), kind=kOutput, calls=%fused_computation.9 | convolution fusion | flops 2148007936 | bytes 7340032 | tf_op jit(solution)/shard_map/dot_general | solution.py:129
  102.7 45.1 %all-gather.9.cloned.1.call-done = bf16[2048,512]{1,0:T(8,128)(2,1)} async-done(((bf16[256,512]{1,0:T(8,128)(2,1)}), bf16[2048,512]{1,0:T(8,128)(2,1)}) %all-gather.9.cloned.1.call-update) | async-done | bytes 2097168 | tf_op jit(solution)/shard_map/all_gather | solution.py:128
  147.8 6.2 %convolution_convert_fusion.4.k_ref = bf16[1024,512]{1,0:T(8,128)(2,1)} fusion(bf16[1024,2048]{1,0:T(8,128)(2,1)} %all-gather.5.cloned.1.call-done, bf16[2048,512]{1,0:T(8,128)(2,1)} %all-gather.9.cloned.1.call-done), kind=kOutput, calls=%fused_computation.8 | convolution fusion | flops 2148007936 | bytes 7340032 | tf_op jit(solution)/shard_map/dot_general | solution.py:129
  154.0 43.5 %all-gather.11.cloned.1.call-done = bf16[2048,512]{1,0:T(8,128)(2,1)} async-done(((bf16[256,512]{1,0:T(8,128)(2,1)}), bf16[2048,512]{1,0:T(8,128)(2,1)}) %all-gather.11.cloned.1.call-update) | async-done | bytes 2097168 | tf_op jit(solution)/shard_map/all_gather | solution.py:128
  197.4 6.2 %convolution_convert_fusion.3.v_ref = bf16[1024,512]{1,0:T(8,128)(2,1)} fusion(bf16[1024,2048]{1,0:T(8,128)(2,1)} %all-gather.5.cloned.1.call-done, bf16[2048,512]{1,0:T(8,128)(2,1)} %all-gather.11.cloned.1.call-done), kind=kOutput, calls=%fused_computation.7 | convolution fusion | flops 2148007936 | bytes 7340032 | tf_op jit(solution)/shard_map/dot_general | solution.py:129
  203.6 6.6 %shard_map.102 = f32[4,4,128,128]{3,2,1,0:T(8,128)} custom-call(bf16[1024,512]{1,0:T(8,128)(2,1)} %convolution_convert_fusion.5.q_ref, bf16[1024,512]{1,0:T(8,128)(2,1)} %convolution_convert_fusion.4.k_ref, bf16[1024,512]{1,0:T(8,128)(2,1)} %convolution_convert_fusion.3.v_ref, bf16[1024,512]{1,0:T(8,128)(2,1)} %g_ref.5, ...), custom_call_target="tpu_custom_call" | custom-call | flops 536870912 | bytes 4194304 | tf_op jit(solution)/shard_map/pallas_call | solution.py:137
  212.3 11.2 %collective-permute-done = bf16[4,4,128,128]{3,2,1,0:T(8,128)(2,1)S(1)} collective-permute-done((bf16[4,4,128,128]{3,2,1,0:T(8,128)(2,1)S(1)}, bf16[4,4,128,128]{3,2,1,0:T(8,128)(2,1)S(1)}, u32[]{:S(2)}, u32[]{:S(2)}) %collective-permute-start) | collective-permute-done | bytes 524320 | tf_op jit(solution)/shard_map/ppermute | solution.py:26
  223.8 2.4 collective-permute-start.1
  226.2 13.6 %shard_map.103 = (f32[1024,512]{1,0:T(8,128)}, f32[1024,512]{1,0:T(8,128)}, f32[1024,512]{1,0:T(8,128)}, f32[1024,512]{1,0:T(8,128)}) custom-call(bf16[1024,512]{1,0:T(8,128)(2,1)} %convolution_convert_fusion.5.q_ref, bf16[1024,512]{1,0:T(8,128)(2,1)} %convolution_convert_fusion.4.k_ref, bf16[1024,512]{1,0:T(8,128)(2,1)} %convolution_convert_fusion.3.v_ref, ...), custom_call_target="tpu_custom_call" | custom-call | flops 3221225472 | bytes 12582912 | tf_op jit(solution)/shard_map/pallas_call | solution.py:148
  240.0 1.5 collective-permute-start.2
  241.5 10.8 %collective-permute-done.2 = bf16[2,4,128,128]{3,2,1,0:T(8,128)(2,1)S(1)} collective-permute-done((bf16[2,4,128,128]{3,2,1,0:T(8,128)(2,1)S(1)}, bf16[2,4,128,128]{3,2,1,0:T(8,128)(2,1)S(1)}, u32[]{:S(2)}, u32[]{:S(2)}) %collective-permute-start.2) | collective-permute-done | bytes 262176 | tf_op jit(solution)/shard_map/ppermute | solution.py:26
  253.9 8.5 %shard_map.104 = (bf16[1024,512]{1,0:T(8,128)(2,1)}, bf16[1024,512]{1,0:T(8,128)(2,1)}, bf16[1024,512]{1,0:T(8,128)(2,1)}, bf16[1024,512]{1,0:T(8,128)(2,1)}) custom-call(bf16[1024,512]{1,0:T(8,128)(2,1)} %convolution_convert_fusion.5.q_ref, bf16[1024,512]{1,0:T(8,128)(2,1)} %convolution_convert_fusion.4.k_ref, ...), custom_call_target="tpu_custom_call" | custom-call | flops 1073741824 | bytes 16777216 | tf_op jit(solution)/shard_map/pallas_call | solution.py:175
  262.4 6.2 %fusion = bf16[2048,512]{0,1:T(8,128)(2,1)} fusion(bf16[1024,512]{1,0:T(8,128)(2,1)} %get-tuple-element.17, bf16[1024,2048]{1,0:T(8,128)(2,1)} %all-gather.5.cloned.1.call-done), kind=kOutput, calls=%fused_computation.3 | convolution fusion | flops 2148532224 | bytes 7340032 | tf_op jit(solution)/shard_map/dot_general | solution.py:16
  269.9 6.0 %fusion.1 = bf16[2048,512]{0,1:T(8,128)(2,1)} fusion(bf16[1024,512]{1,0:T(8,128)(2,1)S(1)} %copy-done.3, bf16[1024,2048]{1,0:T(8,128)(2,1)} %all-gather.5.cloned.1.call-done), kind=kOutput, calls=%fused_computation.4 | convolution fusion | flops 2148532224 | bytes 7340032 | tf_op jit(solution)/shard_map/dot_general | solution.py:16
  277.1 6.0 %fusion.2 = bf16[2048,512]{0,1:T(8,128)(2,1)} fusion(bf16[1024,512]{1,0:T(8,128)(2,1)S(1)} %copy-done.2, bf16[1024,2048]{1,0:T(8,128)(2,1)} %all-gather.5.cloned.1.call-done), kind=kOutput, calls=%fused_computation.5 | convolution fusion | flops 2148532224 | bytes 7340032 | tf_op jit(solution)/shard_map/dot_general | solution.py:16
  283.1 54.0 %reduce-scatter.4.cloned.1.call-done = bf16[256,512]{0,1:T(8,128)(2,1)} async-done(((bf16[2048,512]{0,1:T(8,128)(2,1)}), bf16[256,512]{0,1:T(8,128)(2,1)}) %reduce-scatter.4.cloned.1.call-update) | async-done | bytes 262160 | tf_op jit(solution)/shard_map/reduce_scatter | solution.py:192
  337.1 1.9 copy.19
  338.9 69.6 %reduce-scatter.6.cloned.1.call-done = bf16[256,512]{0,1:T(8,128)(2,1)} async-done(((bf16[2048,512]{0,1:T(8,128)(2,1)}), bf16[256,512]{0,1:T(8,128)(2,1)}) %reduce-scatter.6.cloned.1.call-update) | async-done | bytes 262160 | tf_op jit(solution)/shard_map/reduce_scatter | solution.py:192
  408.5 1.9 copy.20
  410.4 69.7 %reduce-scatter.8.cloned.1.call-done = bf16[256,512]{0,1:T(8,128)(2,1)} async-done(((bf16[2048,512]{0,1:T(8,128)(2,1)}), bf16[256,512]{0,1:T(8,128)(2,1)}) %reduce-scatter.8.cloned.1.call-update) | async-done | bytes 262160 | tf_op jit(solution)/shard_map/reduce_scatter | solution.py:192
  480.1 1.9 copy.21
  (38 shorter events, 9.3 us)
Async XLA Ops:
  7.2 2.9 copy-start
  7.2 54.8 %all-gather.7.cloned.1.call-start = ((), (), s32[]{:S(2)}) async-start(), calls=%async_computation.4 | async-start | bytes 2359296 | tf_op jit(solution)/shard_map/all_gather | solution.py:128
  7.9 88.6 %all-gather.5.cloned.1.call-start = ((), (), s32[]{:S(2)}) async-start(), calls=%async_computation.3 | async-start | bytes 5242880 | tf_op jit(solution)/shard_map/all_gather | solution.py:113
  8.7 139.1 %all-gather.9.cloned.1.call-start = ((), (), s32[]{:S(2)}) async-start(), calls=%async_computation.5 | async-start | bytes 2359296 | tf_op jit(solution)/shard_map/all_gather | solution.py:128
  9.4 188.0 %all-gather.11.cloned.1.call-start = ((), (), s32[]{:S(2)}) async-start(), calls=%async_computation.6 | async-start | bytes 2359296 | tf_op jit(solution)/shard_map/all_gather | solution.py:128
  10.0 327.1 %reduce-scatter.4.cloned.1.call-start = ((), (), s32[]{:S(2)}) async-start(), calls=%async_computation.7 | async-start | bytes 2359296 | tf_op jit(solution)/shard_map/reduce_scatter | solution.py:192
  210.3 13.3 %copy-start.1 = (f32[4,4,128,128]{3,2,1,0:T(8,128)S(1)}, f32[4,4,128,128]{3,2,1,0:T(8,128)}, u32[]{:S(2)}) copy-start(f32[4,4,128,128]{3,2,1,0:T(8,128)} %shard_map.102) | copy-start | bytes 3145732
  211.7 11.8 %collective-permute-start = (bf16[4,4,128,128]{3,2,1,0:T(8,128)(2,1)S(1)}, bf16[4,4,128,128]{3,2,1,0:T(8,128)(2,1)S(1)}, u32[]{:S(2)}, u32[]{:S(2)}) collective-permute-start(bf16[4,4,128,128]{3,2,1,0:T(8,128)(2,1)S(1)} %convert_element_type.71), channel_id=1, source_target_pairs={{0,4},{4,0},{8,12},{12,8},{16,20},{20,16},{24,28},{28,24},{1,5},{5... | collective-permute-start | bytes 1572872 | tf_op jit(solution)/shard_map/ppermute | solution.py:26
  223.8 16.1 %collective-permute-start.1 = (bf16[3,4,128,128]{3,2,1,0:T(8,128)(2,1)S(1)}, bf16[3,4,128,128]{3,2,1,0:T(8,128)(2,1)S(1)}, u32[]{:S(2)}, u32[]{:S(2)}) collective-permute-start(bf16[3,4,128,128]{3,2,1,0:T(8,128)(2,1)S(1)} %pad_maximum_fusion), channel_id=1, source_target_pairs={{0,8},{8,0},{4,12},{12,4},{16,24},{24,16},{20,28},{28,20},{1,9},{9... | collective-permute-start | bytes 1179656 | tf_op jit(solution)/shard_map/ppermute | solution.py:26
  240.0 12.3 %collective-permute-start.2 = (bf16[2,4,128,128]{3,2,1,0:T(8,128)(2,1)S(1)}, bf16[2,4,128,128]{3,2,1,0:T(8,128)(2,1)S(1)}, u32[]{:S(2)}, u32[]{:S(2)}) collective-permute-start(bf16[2,4,128,128]{3,2,1,0:T(8,128)(2,1)S(1)} %pad_maximum_fusion.2), channel_id=1, source_target_pairs={{0,16},{16,0},{4,20},{20,4},{8,24},{24,8},{12,28},{28,12},{1,17},{... | collective-permute-start | bytes 786440 | tf_op jit(solution)/shard_map/ppermute | solution.py:26
  268.6 1.2 copy-start.3
  268.7 139.9 %reduce-scatter.6.cloned.1.call-start = ((), (), s32[]{:S(2)}) async-start(), calls=%async_computation.8 | async-start | bytes 2359296 | tf_op jit(solution)/shard_map/reduce_scatter | solution.py:192
  275.8 1.2 copy-start.2
  275.9 204.2 %reduce-scatter.8.cloned.1.call-start = ((), (), s32[]{:S(2)}) async-start(), calls=%async_computation.9 | async-start | bytes 2359296 | tf_op jit(solution)/shard_map/reduce_scatter | solution.py:192
Sparse Core Ops, SparseCore 0:
  10.1 51.7 all-gather.6
  63.5 32.9 all-gather.4
  98.7 49.0 all-gather.8
  149.8 47.6 all-gather.10
  268.8 68.2 reduce-scatter.3
  340.4 68.0 reduce-scatter.5
  412.1 67.9 reduce-scatter.7
